TPU v7x, 256 devices: a whole 4x4x8 slice. The times are simulated.
256 devices in a mesh: slab: 128 (over z, y_lo, x, core), chan: 2 (over y_hi).
Axes of the slice: x: 4, y: 4 (y_hi: 2, y_lo: 2; y = y_hi * 2 + y_lo), z: 8, core: 2. Of those that a mesh axis runs over, the one named last changes fastest.
Arguments:
- species: int32 [32768], P('slab'), may hold values from 0 to 4
- atom_count: int32 [128], P('slab'), may hold values from 192 to 256, as said below
- halo_index: int32 [128, 2, 128], P('slab'), may hold values from 0 to 255, as said below
- edge_count: int32 [128, 2], P('slab'), may hold values from 512 to 12288, as said below
- inner_edges: int32 [2, 1572864], P(None, 'slab'), may hold values from 0 to 255, as said below
- outer_edges: int32 [2, 524288], P(None, 'slab'), may hold values from 0 to 255, as said below
- inner_vec: float32 [3, 1572864], P(None, 'slab'), may hold values from -4.8 to 4.8, as said below
- outer_vec: float32 [3, 524288], P(None, 'slab'), may hold values from -4.8 to 4.8, as said below
- embed_table: bfloat16 [64, 5], replicated, may hold values from -6 to 6
- radial_in: bfloat16 [2, 64, 8], replicated, may hold values from -2 to 2
- radial_mid: bfloat16 [2, 64, 64], replicated, may hold values from -0.75 to 0.75
- radial_out: bfloat16 [2, 10, 64, 64], P(None, None, 'chan'), may hold values from -0.75 to 0.75
- mix_in: bfloat16 [2, 3, 64, 64], P(None, None, 'chan'), may hold values from -0.75 to 0.75
- mix_scalar: bfloat16 [2, 192, 64], replicated, may hold values from -0.75 to 0.75
- mix_irrep: bfloat16 [2, 2, 64, 64], replicated, may hold values from -0.75 to 0.75
- readout: float32 [64], replicated, may hold values from -0.75 to 0.75
- species_energy: float32 [5], replicated, may hold values from -6 to -2
Outputs:
- node_state: float32 [9, 64, 32768], P(None, None, 'slab')
- atom_energy: float32 [32768], P('slab')
- mean_energy: float32 [], replicated
Inputs may be any that keep to these rules, and one draw needn't show every extreme that they name: `atom_count`: each slab holds between 192 and 256 live atoms (rounded down), live slots first; some slab holds exactly 256. `halo_index`: every entry names a live atom of its own slab. `edge_count`: column 0 lies between 1536 and 12288, column 1 between 512 and 4096 (rounded down); live slots come first in each list; each column reaches its most in some slab. `inner_edges`: both rows name live atoms of the same slab, in every slot. `outer_edges`: row 0 lies below 256; row 1 names a live atom of the slab, in every slot. `inner_vec`: every displacement is shorter than 4.8; nearly all are 0.9 or longer, and a rare few are shorter. `outer_vec`: every displacement is shorter than 4.8; nearly all are 0.9 or longer, and a rare few are shorter.
All inputs are finite; a program needn't handle non-finite values.
Results may differ from a plain program's by a relative error of at most 0.00045.
Values may be sent and summed in bfloat16 or wider, within the bound.
A program may use at most 64 MiB of HBM per device.

v0:
```python
import functools
import math

import jax
import jax.numpy as jnp
from jax import lax
from jax.sharding import Mesh
from jax.experimental import pallas as pl
from jax.experimental.pallas import tpu as pltpu
from jax.sharding import PartitionSpec as P

SLAB = ("slab_0", "slab_1", "slab_2", "slab_3")


cutoff = 5.0
neighbour_norm = 1.0 / math.sqrt(48.0)
half_root = 0.5 * math.sqrt(3.0)


def passed_along(array, axis, by):
    devices = lax.axis_size(axis)
    return lax.ppermute(array, axis, [(i, (i + by) % devices) for i in range(devices)])


def mix_channels(weights, rounded):
    scalar_part = jnp.dot(weights[0], rounded[0], preferred_element_type=jnp.float32)[None]
    vector_part = jnp.einsum(
        "oi,kia->koa", weights[1], rounded[1:4], preferred_element_type=jnp.float32
    )
    tensor_part = jnp.einsum(
        "oi,kia->koa", weights[2], rounded[4:9], preferred_element_type=jnp.float32
    )
    return jnp.concatenate([scalar_part, vector_part, tensor_part], axis=0)


def gate_update(aggregated, scalar_weight, irrep_weight):
    channels = aggregated.shape[1]
    mixed_scalar = jnp.dot(scalar_weight, aggregated[0], preferred_element_type=jnp.float32)
    mixed_vector = jnp.einsum(
        "oi,kia->koa", irrep_weight[0], aggregated[1:4], preferred_element_type=jnp.float32
    )
    mixed_tensor = jnp.einsum(
        "oi,kia->koa", irrep_weight[1], aggregated[4:9], preferred_element_type=jnp.float32
    )
    new_scalar = jax.nn.silu(mixed_scalar[:channels])[None]
    new_vector = jax.nn.sigmoid(mixed_scalar[channels : 2 * channels])[None] * mixed_vector
    new_tensor = jax.nn.sigmoid(mixed_scalar[2 * channels :])[None] * mixed_tensor
    return jnp.concatenate([new_scalar, new_vector, new_tensor], axis=0)


def sine_of_pi_times(turns):
    nearest = jnp.round(turns)
    rest = turns - nearest
    half = 0.5 * nearest
    sign = 1.0 - 4.0 * (half - jnp.floor(half))
    square = rest * rest
    series = jnp.float32(-0.0073704309)
    series = series * square + 0.08214588661112823
    series = series * square - 0.5992645293207921
    series = series * square + 2.550164039877345
    series = series * square - 5.16771278004997
    series = series * square + 3.141592653589793
    return series * (rest * sign)


def silu_of_twice(half):
    return half + half * jnp.tanh(half)


def radial_kernel(count_ref, vec_ref, first_ref, middle_ref, hidden_ref, unit_ref, *, column, block):
    orders = (lax.broadcasted_iota(jnp.int32, (8, 1), 0) + 1).astype(jnp.float32)

    def visit(index, carry):
        span = pl.ds(pl.multiple_of(index * block, block), block)
        vec = vec_ref[:, span]
        x, y, z = vec[0:1], vec[1:2], vec[2:3]
        squared = x * x + y * y + z * z
        length = jnp.sqrt(squared)
        inverse = lax.rsqrt(squared + 0.25)
        fraction = jnp.minimum(length * (1.0 / cutoff), 1.0)
        cubed = fraction * fraction * fraction
        envelope = 1.0 + cubed * cubed * (-28.0 + fraction * (48.0 - 21.0 * fraction))
        height = math.sqrt(2.0 / cutoff) * inverse * envelope
        bessel = sine_of_pi_times(orders * (length * (1.0 / cutoff))) * height
        unit_ref[0:1, span] = x * inverse
        unit_ref[1:2, span] = y * inverse
        unit_ref[2:3, span] = z * inverse
        hidden = silu_of_twice(
            jnp.dot(first_ref[...], bessel.astype(jnp.bfloat16), preferred_element_type=jnp.float32)
        ).astype(jnp.bfloat16)
        hidden_ref[:, span] = silu_of_twice(
            jnp.dot(middle_ref[...], hidden, preferred_element_type=jnp.float32)
        ).astype(jnp.bfloat16)
        return carry

    lax.fori_loop(0, (count_ref[0, column] + block - 1) // block, visit, 0)


def radial_net(edge_count, vec, first, middle, column):
    slots = vec.shape[1]
    in_vmem = pl.BlockSpec(memory_space=pltpu.VMEM)
    return pl.pallas_call(
        functools.partial(radial_kernel, column=column, block=min(2048, slots)),
        out_shape=(
            jax.ShapeDtypeStruct((middle.shape[0], slots), jnp.bfloat16),
            jax.ShapeDtypeStruct((8, slots), jnp.float32),
        ),
        in_specs=[pl.BlockSpec(memory_space=pltpu.SMEM)] + [in_vmem] * 3,
        out_specs=(in_vmem, in_vmem),
        compiler_params=pltpu.CompilerParams(vmem_limit_bytes=40 * 2**20),
        cost_estimate=pl.CostEstimate(
            flops=slots * 40000, bytes_accessed=slots * 300, transcendentals=0
        ),
    )(edge_count, vec, first, middle)


def edge_kernel(
    count_ref,
    table_ref,
    edges_ref,
    hidden_ref,
    unit_ref,
    mix_ref,
    *rest,
    column,
    block,
    channels,
    first_row,
    last,
):
    if last:
        before_ref, out_ref, *scratch = rest
    else:
        out_ref, *scratch = rest
    weight_sc, source_sc, message_sc, direction_sc = (scratch[2 * k : 2 * k + 2] for k in range(4))
    target_sc, sum_sc = scratch[8:]
    count = count_ref[0, column]
    blocks = (count + block - 1) // block
    slots = edges_ref.shape[1]
    rows, atoms = table_ref.shape
    breadth = mix_ref.shape[1]
    sum_sc[...] = jnp.zeros_like(sum_sc)
    message_sc[1][...] = jnp.zeros_like(message_sc[1])
    names = lax.broadcasted_iota(jnp.int32, (atoms, 1), 0).astype(jnp.float32).astype(jnp.bfloat16)
    one = jnp.ones((), jnp.bfloat16)
    zero = jnp.zeros((), jnp.bfloat16)

    def span_of(index):
        start = jnp.clip(index * block, 0, slots - block)
        return pl.ds(pl.multiple_of(start, block), block)

    def expansion(index, into):
        span = span_of(index)
        source = edges_ref[0:1, span].astype(jnp.float32).astype(jnp.bfloat16)
        hidden = hidden_ref[first_row : first_row + breadth, span]
        direction_sc[into][0:3, :] = unit_ref[0:3, span]

        def gather(lane):
            cut = slice(lane, lane + 256)
            onehot = jnp.where(names == source[:, cut], one, zero)
            source_sc[into][:, cut] = jnp.dot(
                table_ref[...], onehot, preferred_element_type=jnp.float32
            )

        def weigh(lane):
            cut = slice(lane, lane + 256)
            weight_sc[into][:, cut] = jnp.dot(
                mix_ref[...], hidden[:, cut], preferred_element_type=jnp.float32
            )

        lanes = range(0, block, 256)
        return [functools.partial(gather, k) for k in lanes] + [
            functools.partial(weigh, k) for k in lanes
        ]

    def reduction(index, held):
        place = lax.broadcasted_iota(jnp.int32, (1, block), 1) + index * block
        target = jnp.where(place < count, edges_ref[1:2, span_of(index)], -1)
        target = target.astype(jnp.float32).astype(jnp.bfloat16)
        for lane in range(0, block, 256):
            cut = slice(lane, lane + 256)
            target_sc[:, cut] = jnp.where(names == target[:, cut], one, zero)

        def scatter(row):
            cut = slice(row, row + rows)
            sum_sc[cut, :] += lax.dot_general(
                message_sc[held][cut, :],
                target_sc[...],
                (((1,), (1,)), ((), ())),
                preferred_element_type=jnp.float32,
            )

        return [functools.partial(scatter, 0), functools.partial(scatter, rows)]

    def messages(held, lane, group):
        span = slice(lane, lane + 256)
        x, y, z = (
            jnp.broadcast_to(direction_sc[held][k : k + 1, span], (8, 256)) for k in range(3)
        )
        hx, hy, hz = half_root * x, half_root * y, half_root * z

        def feature(k):
            return source_sc[held][k * channels + group : k * channels + group + 8, span]

        def weight(p):
            return weight_sc[held][p * channels + group : p * channels + group + 8, span]

        def put(k, value):
            upper = value.astype(jnp.bfloat16)
            lower = (value - upper.astype(jnp.float32)).astype(jnp.bfloat16)
            row = k * channels + group
            message_sc[held][row : row + 8, span] = upper
            message_sc[held][rows + row : rows + row + 8, span] = lower

        t1, t2, t3, t4, t5 = (feature(k) for k in range(4, 9))
        t5_part, t3_part = half_root * t5, 0.5 * t3
        g1 = hy * t1 + hz * t4 + x * (t5_part - t3_part)
        g2 = hx * t1 + hz * t2 - y * (t5_part + t3_part)
        g3 = hy * t2 + hx * t4 + z * t3
        v1, v2, v3 = (feature(k) for k in range(1, 4))
        s = feature(0)
        put(
            0,
            weight(0) * s
            + weight(1) * (x * g1 + y * g2 + z * g3)
            + weight(2) * (x * v1 + y * v2 + z * v3),
        )
        a = weight(3) * s
        w4, w5, w6 = weight(4), weight(5), weight(6)
        p1, p2, p3 = w5 * v1, w5 * v2, w5 * v3
        put(1, a * x + w4 * v1 + (p2 * z - p3 * y) + w6 * g1)
        put(2, a * y + w4 * v2 + (p3 * x - p1 * z) + w6 * g2)
        put(3, a * z + w4 * v3 + (p1 * y - p2 * x) + w6 * g3)
        a = weight(7) * s
        w8, w9 = weight(8), weight(9)
        p1, p2, p3 = w9 * v1 + a * x, w9 * v2 + a * y, w9 * v3 + a * z
        put(4, w8 * t1 + (hy * p1 + hx * p2))
        put(5, w8 * t2 + (hz * p2 + hy * p3))
        put(6, w8 * t3 + (z * p3 - 0.5 * (x * p1 + y * p2)))
        put(7, w8 * t4 + (hz * p1 + hx * p3))
        put(8, w8 * t5 + (hx * p1 - hy * p2))

    def stage(index, held):
        pieces = expansion(index + 1, 1 - held) + reduction(index - 1, 1 - held)
        units = [(lane, group) for lane in range(0, block, 256) for group in range(0, channels, 8)]
        done = 0
        for position, unit in enumerate(units):
            while done < len(pieces) and done * len(units) * 4 < (position + 1) * len(pieces) * 5:
                pieces[done]()
                done += 1
            messages(held, *unit)

    def drain(held):
        for piece in reduction(blocks - 1, held):
            piece()

    for piece in expansion(0, 0):
        piece()

    def visit(index, carry):
        pl.when(2 * index < blocks)(lambda: stage(2 * index, 0))
        pl.when(2 * index + 1 < blocks)(lambda: stage(2 * index + 1, 1))
        return carry

    lax.fori_loop(0, (blocks + 1) // 2, visit, 0)
    odd = lax.rem(blocks, 2)
    pl.when(odd == 1)(lambda: drain(0))
    pl.when(odd == 0)(lambda: drain(1))
    total = sum_sc[0:rows, :] + sum_sc[rows : 2 * rows, :]
    if last:
        total = (total + before_ref[...]) * neighbour_norm
    out_ref[...] = total.astype(out_ref.dtype)


def sum_edges(edge_count, table, edges, hidden, unit, mix, layer_index, column, before=None):
    rows, atoms = table.shape
    slots = edges.shape[1]
    last = before is not None
    block = min(512 if last else 1024, slots)
    paths, breadth = mix.shape
    in_vmem = pl.BlockSpec(memory_space=pltpu.VMEM)
    arrays = [edge_count, table, edges, hidden, unit, mix]
    if last:
        arrays.append(before)

    def two(shape, dtype):
        return [pltpu.VMEM(shape, dtype)] * 2

    return pl.pallas_call(
        functools.partial(
            edge_kernel,
            column=column,
            block=block,
            channels=rows // 9,
            first_row=layer_index * breadth,
            last=last,
        ),
        out_shape=jax.ShapeDtypeStruct((rows, atoms), jnp.bfloat16 if last else jnp.float32),
        in_specs=[pl.BlockSpec(memory_space=pltpu.SMEM)] + [in_vmem] * (len(arrays) - 1),
        out_specs=in_vmem,
        scratch_shapes=two((paths, block), jnp.float32)
        + two((rows, block), jnp.float32)
        + two((2 * rows, block), jnp.bfloat16)
        + two((8, block), jnp.float32)
        + [pltpu.VMEM((atoms, block), jnp.bfloat16), pltpu.VMEM((2 * rows, atoms), jnp.float32)],
        compiler_params=pltpu.CompilerParams(vmem_limit_bytes=40 * 2**20),
        cost_estimate=pl.CostEstimate(
            flops=slots * 400000, bytes_accessed=slots * 300, transcendentals=0
        ),
    )(*arrays)


def total_kernel(part_ref, total_ref, near_sc, far_sc, near_send, near_recv, far_send, far_recv):
    far, *near = SLAB
    sizes = [lax.axis_size(name) for name in near]
    place = [lax.axis_index(name) for name in near]
    far_size = lax.axis_size(far)
    far_place = lax.axis_index(far)
    near_total = math.prod(sizes)

    def split(step):
        return step // (sizes[1] * sizes[2]), step // sizes[2] % sizes[1], step % sizes[2]

    def near_device(step):
        return {
            name: (at + by) % size for name, at, by, size in zip(near, place, split(step), sizes)
        }

    def near_sender(step):
        at = [(p + size - by) % size for p, by, size in zip(place, split(step), sizes)]
        return (at[0] * sizes[1] + at[1]) * sizes[2] + at[2]

    def near_copy(step, slot):
        return pltpu.make_async_remote_copy(
            src_ref=part_ref,
            dst_ref=near_sc.at[slot],
            send_sem=near_send.at[step],
            recv_sem=near_recv.at[slot],
            device_id=near_device(step),
            device_id_type=pl.DeviceIdType.MESH,
        )

    def far_copy(step, slot):
        return pltpu.make_async_remote_copy(
            src_ref=near_sc,
            dst_ref=far_sc.at[slot],
            send_sem=far_send.at[step],
            recv_sem=far_recv.at[slot],
            device_id={far: (far_place + step) % far_size},
            device_id_type=pl.DeviceIdType.MESH,
        )

    barrier = pltpu.get_barrier_semaphore()
    for step in range(1, near_total):
        pl.semaphore_signal(
            barrier, inc=1, device_id=near_device(step), device_id_type=pl.DeviceIdType.MESH
        )
    for step in range(1, far_size):
        pl.semaphore_signal(
            barrier,
            inc=1,
            device_id={far: (far_place + step) % far_size},
            device_id_type=pl.DeviceIdType.MESH,
        )
    pl.semaphore_wait(barrier, near_total + far_size - 2)
    mine = near_sender(0)
    near_sc[mine] = part_ref[...]
    for step in range(1, near_total):
        near_copy(step, mine).start()
    for step in range(1, near_total):
        near_copy(step, near_sender(step)).wait_recv()
    for step in range(1, far_size):
        far_copy(step, far_place).start()
    far_sc[far_place] = near_sc[...]
    for step in range(1, far_size):
        far_copy(step, (far_place + far_size - step) % far_size).wait_recv()
    total_ref[...] = jnp.sum(far_sc[...], axis=(0, 1))
    for step in range(1, near_total):
        near_copy(step, mine).wait_send()
    for step in range(1, far_size):
        far_copy(step, far_place).wait_send()


def total_over_slabs(part):
    lanes = part.shape[1]
    far_size, near_total = lax.axis_size(SLAB[0]), lax.axis_size(SLAB[1:])
    return pl.pallas_call(
        total_kernel,
        out_shape=jax.ShapeDtypeStruct((1, lanes), jnp.float32),
        in_specs=[pl.BlockSpec(memory_space=pltpu.VMEM)],
        out_specs=pl.BlockSpec(memory_space=pltpu.VMEM),
        scratch_shapes=[
            pltpu.VMEM((near_total, 1, lanes), jnp.float32),
            pltpu.VMEM((far_size, near_total, 1, lanes), jnp.float32),
            pltpu.SemaphoreType.DMA((near_total,)),
            pltpu.SemaphoreType.DMA((near_total,)),
            pltpu.SemaphoreType.DMA((far_size,)),
            pltpu.SemaphoreType.DMA((far_size,)),
        ],
        compiler_params=pltpu.CompilerParams(collective_id=0, has_side_effects=True),
    )(part)


def local(
    species,
    atom_count,
    halo_index,
    edge_count,
    inner_edges,
    outer_edges,
    inner_vec,
    outer_vec,
    embed_table,
    radial_in,
    radial_mid,
    radial_out,
    mix_in,
    mix_scalar,
    mix_irrep,
    readout,
    species_energy,
):
    atom_total = species.shape[0]
    species_total = embed_table.shape[1]
    onehot = species[None, :] == jnp.arange(species_total, dtype=jnp.int32)[:, None]
    scalar_init = jnp.dot(
        embed_table, onehot.astype(jnp.bfloat16), preferred_element_type=jnp.float32
    )
    node_state = jnp.concatenate(
        [scalar_init[None], jnp.zeros((8,) + scalar_init.shape, jnp.float32)], axis=0
    )
    channels = mix_in.shape[2]
    atom_slots = jnp.arange(atom_total, dtype=jnp.int32)
    to_left, to_right = (
        (atom_slots[:, None] == halo_index[0, side][None, :]).astype(jnp.bfloat16)
        for side in (0, 1)
    )
    first = lax.axis_index("chan") == 0
    layers, breadth, _ = radial_in.shape
    first_weights = (radial_in * 0.5).reshape(layers * breadth, -1)
    middle_weights = jnp.zeros((layers * breadth, layers * breadth), jnp.bfloat16)
    for layer_index in range(layers):
        cut = slice(layer_index * breadth, (layer_index + 1) * breadth)
        middle_weights = middle_weights.at[cut, cut].set(radial_mid[layer_index] * 0.5)
    for layer_index in range(layers):
        rounded = node_state.astype(jnp.bfloat16)
        features = mix_channels(mix_in[layer_index], rounded).astype(jnp.bfloat16)
        table = features.reshape(9 * channels, atom_total)
        mix = radial_out[layer_index].reshape(-1, breadth)

        def boundary(choice):
            return jnp.dot(table, choice, preferred_element_type=jnp.float32).astype(jnp.bfloat16)

        from_left = passed_along(boundary(to_right), SLAB, 1)
        from_right = passed_along(boundary(to_left), SLAB, -1)
        if layer_index == 0:
            inner_net = radial_net(edge_count, inner_vec, first_weights, middle_weights, 0)
            outer_net = radial_net(edge_count, outer_vec, first_weights, middle_weights, 1)
        summed = sum_edges(edge_count, table, inner_edges, *inner_net, mix, layer_index, 0)
        halo_table = jnp.concatenate([from_left, from_right], axis=1)
        aggregated = sum_edges(
            edge_count, halo_table, outer_edges, *outer_net, mix, layer_index, 1, summed
        ).reshape(9, channels, atom_total)
        other = lax.ppermute(aggregated, "chan", [(0, 1), (1, 0)])
        all_channels = jnp.concatenate(
            [jnp.where(first, aggregated, other), jnp.where(first, other, aggregated)], axis=1
        )
        node_state = node_state + gate_update(
            all_channels, mix_scalar[layer_index], mix_irrep[layer_index]
        )
    readout_part = jnp.sum(node_state[0] * readout[:, None], axis=0)
    species_part = jnp.sum(onehot.astype(jnp.float32) * species_energy[:, None], axis=0)
    live_atoms = (jnp.arange(atom_total, dtype=jnp.int32) < atom_count[0]).astype(jnp.float32)
    atom_energy = (readout_part + species_part) * live_atoms
    energy_sum = jnp.sum(total_over_slabs(jnp.sum(atom_energy.reshape(-1, 128), axis=0)[None]))
    mean_energy = energy_sum / (atom_total * lax.axis_size(SLAB))
    return (node_state, atom_energy, mean_energy)


def solution(mesh):
    finer = Mesh(
        mesh.devices.reshape(8, 2, 4, 2, mesh.shape["chan"]),
        ("slab_0", "slab_1", "slab_2", "slab_3", "chan"),
    )
    placed = (
        P(SLAB),
        P(SLAB),
        P(SLAB, None, None),
        P(SLAB, None),
        P(None, SLAB),
        P(None, SLAB),
        P(None, SLAB),
        P(None, SLAB),
        P(),
        P(),
        P(),
        P(None, None, "chan", None),
        P(None, None, "chan", None),
        P(),
        P(),
        P(),
        P(),
    )
    return jax.shard_map(
        local,
        mesh=finer,
        in_specs=placed,
        out_specs=(P(None, None, SLAB), P(SLAB), P()),
        check_vma=False,
    )
```

profile of v0, /device:TPU:1, one launch (start us, length us, event | category | flops | bytes accessed | tf_op | source)
XLA Modules:
  0.0 104.0 jit_solution(3681367550562086857)
XLA Ops:
  0.7 0.7 copy-done
  1.3 0.9 convolution_bitcast_fusion.6
  2.2 0.8 fusion.4
  3.1 0.8 fusion.6
  3.9 0.8 fusion.8
  4.7 0.8 slice_bitcast_fusion.6
  5.7 2.7 %collective-permute-start = (bf16[288,128]{1,0:T(8,128)(2,1)S(1)}, bf16[288,128]{1,0:T(8,128)(2,1)S(1)}, u32[]{:S(2)}, u32[]{:S(2)}) collective-permute-start(bf16[288,128]{1,0:T(8,128)(2,1)S(1)} %convolution_convert_fusion.5), channel_id=1, source_target_pairs={{0,2},{2,4},{4,6},{6,8},{8,10},{10,12},{12,14},{14,16},{16,18},{18... | collective-permute-start | bytes 221192 | tf_op jit(solution)/shard_map/ppermute | solution.py:22
  8.6 0.7 collective-permute-start.1
  9.3 0.7 multiply_bitcast_fusion.2
  10.0 0.7 broadcast_multiply_fusion
  10.8 0.9 fusion.77
  11.8 0.7 scatter.9.middle_ref
  12.5 0.9 copy-done.1
  13.5 0.7 copy-done.5
  14.1 1.6 %shard_map.185 = (bf16[128,12288]{1,0:T(8,128)(2,1)S(1)}, f32[8,12288]{1,0:T(8,128)S(1)}) custom-call(s32[1,2]{1,0:T(1,128)S(1)} %copy-done.5, f32[3,12288]{1,0:T(4,128)S(1)} %copy-done.1, bf16[128,8]{1,0:T(8,128)(2,1)S(1)} %bitcast.154, bf16[128,128]{1,0:T(8,128)(2,1)S(1)} %scatter.9.middle_ref), custom_call_target="tpu_custom_call" | custom-call | flops 491520000 | bytes 3686400 | tf_op jit(solution)/shard_map/pallas_call | solution.py:102
  15.7 6.6 %shard_map.186.rest_0_ = f32[288,256]{1,0:T(8,128)S(1)} custom-call(s32[1,2]{1,0:T(1,128)S(1)} %copy-done.5, bf16[288,256]{1,0:T(8,128)(2,1)S(1)} %bitcast.142, s32[2,12288]{1,0:T(2,128)S(1)} %copy-done.2, bf16[128,12288]{1,0:T(8,128)(2,1)S(1)} %get-tuple-element.33.hidden_ref, f32[8,12288]{1,0:T(8,128)S(1)} %get-tuple-element.34.unit_ref, ...), custom_call_target="tpu_custom_call" | custom-call | flops 4915200000 | bytes 3686400 | tf_op jit(solution)/shard_map/pallas_call | solution.py:289
  22.3 1.1 %shard_map.184 = (bf16[128,4096]{1,0:T(8,128)(2,1)S(1)}, f32[8,4096]{1,0:T(8,128)S(1)}) custom-call(s32[1,2]{1,0:T(1,128)S(1)} %copy-done.5, f32[3,4096]{1,0:T(4,128)S(1)} %copy-done.3, bf16[128,8]{1,0:T(8,128)(2,1)S(1)} %bitcast.155, bf16[128,128]{1,0:T(8,128)(2,1)S(1)} %scatter.9.middle_ref), custom_call_target="tpu_custom_call" | custom-call | flops 163840000 | bytes 1228800 | tf_op jit(solution)/shard_map/pallas_call | solution.py:102
  23.5 4.1 %shard_map.187 = bf16[288,256]{1,0:T(8,128)(2,1)S(1)} custom-call(s32[1,2]{1,0:T(1,128)S(1)} %copy-done.5, bf16[288,256]{1,0:T(8,128)(2,1)S(1)} %pad_maximum_fusion.5.table_ref, s32[2,4096]{1,0:T(2,128)S(1)} %copy-done.4, bf16[128,4096]{1,0:T(8,128)(2,1)S(1)} %get-tuple-element.31.hidden_ref, f32[8,4096]{1,0:T(8,128)S(1)} %get-tuple-element.32.unit_ref, ...), custom_call_target="tpu_custom_call" | custom-call | flops 1638400000 | bytes 1228800 | tf_op jit(solution)/shard_map/pallas_call | solution.py:289
  27.6 2.4 %collective-permute-start.2 = (bf16[9,32,256]{2,1,0:T(8,128)(2,1)S(1)}, bf16[9,32,256]{2,1,0:T(8,128)(2,1)S(1)}, u32[]{:S(2)}, u32[]{:S(2)}) collective-permute-start(bf16[9,32,256]{2,1,0:T(8,128)(2,1)S(1)} %bitcast.146), channel_id=1, source_target_pairs={{0,1},{1,0},{2,3},{3,2},{4,5},{5,4},{6,7},{7,6},{8,9},{9,8},{10,11... | collective-permute-start | bytes 442376 | tf_op jit(solution)/shard_map/ppermute | solution.py:464
  30.0 3.2 %collective-permute-done.2 = bf16[9,32,256]{2,1,0:T(8,128)(2,1)S(1)} collective-permute-done((bf16[9,32,256]{2,1,0:T(8,128)(2,1)S(1)}, bf16[9,32,256]{2,1,0:T(8,128)(2,1)S(1)}, u32[]{:S(2)}, u32[]{:S(2)}) %collective-permute-start.2) | collective-permute-done | bytes 147488 | tf_op jit(solution)/shard_map/ppermute | solution.py:464
  33.2 0.2 convolution_bitcast_fusion.5
  34.7 8.9 %collective-permute-start.3 = (bf16[288,128]{1,0:T(8,128)(2,1)S(1)}, bf16[288,128]{1,0:T(8,128)(2,1)S(1)}, u32[]{:S(2)}, u32[]{:S(2)}) collective-permute-start(bf16[288,128]{1,0:T(8,128)(2,1)S(1)} %convolution_convert_fusion.3), channel_id=1, source_target_pairs={{0,2},{2,4},{4,6},{6,8},{8,10},{10,12},{12,14},{14,16},{16,18},{18... | collective-permute-start | bytes 221192 | tf_op jit(solution)/shard_map/ppermute | solution.py:22
  43.6 0.4 collective-permute-start.4
  44.1 6.7 %shard_map.188.rest_0_ = f32[288,256]{1,0:T(8,128)S(1)} custom-call(s32[1,2]{1,0:T(1,128)S(1)} %copy-done.6, bf16[288,256]{1,0:T(8,128)(2,1)S(1)} %bitcast.145, s32[2,12288]{1,0:T(2,128)S(1)} %copy-done.2, bf16[128,12288]{1,0:T(8,128)(2,1)S(1)} %copy-done.8, f32[8,12288]{1,0:T(8,128)S(1)} %get-tuple-element.34.unit_ref, bf16[320,64]{1,0:T(8,128)(2,1)S(1)} %bitcast.150), custom_call_target="tpu_custom_call" | custom-call | flops 4915200000 | bytes 3686400 | tf_op jit(solution)/shard_map/pallas_call | solution.py:289
  50.9 4.0 %shard_map.189 = bf16[288,256]{1,0:T(8,128)(2,1)S(1)} custom-call(s32[1,2]{1,0:T(1,128)S(1)} %copy-done.6, bf16[288,256]{1,0:T(8,128)(2,1)S(1)} %pad_maximum_fusion.7.table_ref, s32[2,4096]{1,0:T(2,128)S(1)} %copy-done.4, bf16[128,4096]{1,0:T(8,128)(2,1)S(1)} %get-tuple-element.31.hidden_ref, f32[8,4096]{1,0:T(8,128)S(1)} %get-tuple-element.32.unit_ref, ...), custom_call_target="tpu_custom_call" | custom-call | flops 1638400000 | bytes 1228800 | tf_op jit(solution)/shard_map/pallas_call | solution.py:289
  54.9 2.7 %collective-permute-start.5 = (bf16[9,32,256]{2,1,0:T(8,128)(2,1)S(1)}, bf16[9,32,256]{2,1,0:T(8,128)(2,1)S(1)}, u32[]{:S(2)}, u32[]{:S(2)}) collective-permute-start(bf16[9,32,256]{2,1,0:T(8,128)(2,1)S(1)} %bitcast.148), channel_id=1, source_target_pairs={{0,1},{1,0},{2,3},{3,2},{4,5},{5,4},{6,7},{7,6},{8,9},{9,8},{10,11... | collective-permute-start | bytes 442376 | tf_op jit(solution)/shard_map/ppermute | solution.py:464
  58.4 2.1 %collective-permute-done.5 = bf16[9,32,256]{2,1,0:T(8,128)(2,1)S(1)} collective-permute-done((bf16[9,32,256]{2,1,0:T(8,128)(2,1)S(1)}, bf16[9,32,256]{2,1,0:T(8,128)(2,1)S(1)}, u32[]{:S(2)}, u32[]{:S(2)}) %collective-permute-start.5) | collective-permute-done | bytes 147488 | tf_op jit(solution)/shard_map/ppermute | solution.py:464
  60.5 0.2 convolution_bitcast_fusion.4
  61.4 0.6 fusion.70
  62.0 38.4 %shard_map.190 = f32[1,128]{1,0:T(1,128)} custom-call(f32[1,128]{1,0:T(1,128)} %bitcast.156), custom_call_target="tpu_custom_call" | custom-call | tf_op jit(solution)/shard_map/pallas_call | solution.py:387
  100.4 0.6 compare_select_fusion.1
  100.9 1.3 %reduce_sum.39 = f32[]{:T(128)} reduce(f32[1,128]{1,0:T(1,128)} %shard_map.190, f32[]{:T(128)} %constant.69.clone.1), dimensions={0,1}, to_apply=%region_3.4 | reduce | flops 127 | bytes 520 | tf_op jit(solution)/shard_map/reduce_sum | solution.py:475
  (59 shorter events, 2.6 us)
Async XLA Ops:
  0.6 0.7 copy-start
  0.6 15.0 %copy-start.2 = (s32[2,12288]{1,0:T(2,128)S(1)}, s32[2,12288]{1,0:T(2,128)}, u32[]{:S(2)}) copy-start(s32[2,12288]{1,0:T(2,128)} %edges_ref.6) | copy-start | bytes 294916
  5.7 17.7 %collective-permute-start = (bf16[288,128]{1,0:T(8,128)(2,1)S(1)}, bf16[288,128]{1,0:T(8,128)(2,1)S(1)}, u32[]{:S(2)}, u32[]{:S(2)}) collective-permute-start(bf16[288,128]{1,0:T(8,128)(2,1)S(1)} %convolution_convert_fusion.5), channel_id=1, source_target_pairs={{0,2},{2,4},{4,6},{6,8},{8,10},{10,12},{12,14},{14,16},{16,18},{18... | collective-permute-start | bytes 221192 | tf_op jit(solution)/shard_map/ppermute | solution.py:22
  8.6 14.8 %collective-permute-start.1 = (bf16[288,128]{1,0:T(8,128)(2,1)S(1)}, bf16[288,128]{1,0:T(8,128)(2,1)S(1)}, u32[]{:S(2)}, u32[]{:S(2)}) collective-permute-start(bf16[288,128]{1,0:T(8,128)(2,1)S(1)} %convolution_convert_fusion.4), channel_id=1, source_target_pairs={{0,254},{2,0},{4,2},{6,4},{8,6},{10,8},{12,10},{14,12},{16,14},{18... | collective-permute-start | bytes 221192 | tf_op jit(solution)/shard_map/ppermute | solution.py:22
  12.5 0.9 copy-start.1
  13.5 0.7 copy-start.5
  15.7 6.6 %copy-start.7 = (bf16[128,12288]{1,0:T(8,128)(2,1)}, bf16[128,12288]{1,0:T(8,128)(2,1)S(1)}, u32[]{:S(2)}) copy-start(bf16[128,12288]{1,0:T(8,128)(2,1)S(1)} %get-tuple-element.33.hidden_ref) | copy-start | bytes 9437188
  15.7 6.6 %copy-start.3 = (f32[3,4096]{1,0:T(4,128)S(1)}, f32[3,4096]{1,0:T(4,128)}, u32[]{:S(2)}) copy-start(f32[3,4096]{1,0:T(4,128)} %vec_ref.2) | copy-start | bytes 147460
  15.7 7.7 %copy-start.4 = (s32[2,4096]{1,0:T(2,128)S(1)}, s32[2,4096]{1,0:T(2,128)}, u32[]{:S(2)}) copy-start(s32[2,4096]{1,0:T(2,128)} %edges_ref.7) | copy-start | bytes 98308
  23.4 9.7 %copy-start.10 = (bf16[2,192,64]{1,2,0:T(8,128)(2,1)S(1)}, bf16[2,192,64]{1,2,0:T(8,128)(2,1)}, u32[]{:S(2)}) copy-start(bf16[2,192,64]{1,2,0:T(8,128)(2,1)} %param.34) | copy-start | bytes 147460
  23.5 10.0 %copy-start.11 = (bf16[2,2,64,64]{3,2,1,0:T(8,128)(2,1)S(1)}, bf16[2,2,64,64]{3,2,1,0:T(8,128)(2,1)}, u32[]{:S(2)}) copy-start(bf16[2,2,64,64]{3,2,1,0:T(8,128)(2,1)} %param.35) | copy-start | bytes 98308
  27.5 6.4 %copy-start.12 = (bf16[2,3,32,64]{3,2,1,0:T(8,128)(2,1)S(1)}, bf16[2,3,32,64]{3,2,1,0:T(8,128)(2,1)}, u32[]{:S(2)}) copy-start(bf16[2,3,32,64]{3,2,1,0:T(8,128)(2,1)} %param.33) | copy-start | bytes 73732
  27.5 16.5 %copy-start.6 = (s32[1,2]{1,0:T(1,128)S(1)}, s32[1,2]{1,0:T(1,128)}, u32[]{:S(2)}) copy-start(s32[1,2]{1,0:T(1,128)} %count_ref.11) | copy-start | bytes 28
  27.6 5.6 %collective-permute-start.2 = (bf16[9,32,256]{2,1,0:T(8,128)(2,1)S(1)}, bf16[9,32,256]{2,1,0:T(8,128)(2,1)S(1)}, u32[]{:S(2)}, u32[]{:S(2)}) collective-permute-start(bf16[9,32,256]{2,1,0:T(8,128)(2,1)S(1)} %bitcast.146), channel_id=1, source_target_pairs={{0,1},{1,0},{2,3},{3,2},{4,5},{5,4},{6,7},{7,6},{8,9},{9,8},{10,11... | collective-permute-start | bytes 442376 | tf_op jit(solution)/shard_map/ppermute | solution.py:464
  30.0 14.1 %copy-start.8 = (bf16[128,12288]{1,0:T(8,128)(2,1)S(1)}, bf16[128,12288]{1,0:T(8,128)(2,1)}, u32[]{:S(2)}) copy-start(bf16[128,12288]{1,0:T(8,128)(2,1)} %copy-done.7) | copy-start | bytes 9437188
  34.7 16.1 %collective-permute-start.3 = (bf16[288,128]{1,0:T(8,128)(2,1)S(1)}, bf16[288,128]{1,0:T(8,128)(2,1)S(1)}, u32[]{:S(2)}, u32[]{:S(2)}) collective-permute-start(bf16[288,128]{1,0:T(8,128)(2,1)S(1)} %convolution_convert_fusion.3), channel_id=1, source_target_pairs={{0,2},{2,4},{4,6},{6,8},{8,10},{10,12},{12,14},{14,16},{16,18},{18... | collective-permute-start | bytes 221192 | tf_op jit(solution)/shard_map/ppermute | solution.py:22
  43.6 7.2 %collective-permute-start.4 = (bf16[288,128]{1,0:T(8,128)(2,1)S(1)}, bf16[288,128]{1,0:T(8,128)(2,1)S(1)}, u32[]{:S(2)}, u32[]{:S(2)}) collective-permute-start(bf16[288,128]{1,0:T(8,128)(2,1)S(1)} %convolution_convert_fusion.2), channel_id=1, source_target_pairs={{0,254},{2,0},{4,2},{6,4},{8,6},{10,8},{12,10},{14,12},{16,14},{18... | collective-permute-start | bytes 221192 | tf_op jit(solution)/shard_map/ppermute | solution.py:22
  50.8 7.5 %copy-start.13 = (s32[256]{0:T(256)S(1)}, s32[256]{0:T(256)}, u32[]{:S(2)}) copy-start(s32[256]{0:T(256)} %param.21) | copy-start | bytes 3076
  50.8 7.5 %copy-start.15 = (f32[5]{0:T(128)S(1)}, f32[5]{0:T(128)}, u32[]{:S(2)}) copy-start(f32[5]{0:T(128)} %param.37) | copy-start | bytes 64
  54.9 6.4 %copy-start.14 = (f32[64]{0:T(128)S(1)}, f32[64]{0:T(128)}, u32[]{:S(2)}) copy-start(f32[64]{0:T(128)} %param.36) | copy-start | bytes 772
  54.9 5.6 %collective-permute-start.5 = (bf16[9,32,256]{2,1,0:T(8,128)(2,1)S(1)}, bf16[9,32,256]{2,1,0:T(8,128)(2,1)S(1)}, u32[]{:S(2)}, u32[]{:S(2)}) collective-permute-start(bf16[9,32,256]{2,1,0:T(8,128)(2,1)S(1)} %bitcast.148), channel_id=1, source_target_pairs={{0,1},{1,0},{2,3},{3,2},{4,5},{5,4},{6,7},{7,6},{8,9},{9,8},{10,11... | collective-permute-start | bytes 442376 | tf_op jit(solution)/shard_map/ppermute | solution.py:464
  61.3 41.6 %copy-start.9 = (f32[9,64,256]{2,1,0:T(8,128)}, f32[9,64,256]{2,1,0:T(8,128)S(1)}, u32[]{:S(2)}) copy-start(f32[9,64,256]{2,1,0:T(8,128)S(1)} %maximum_add_fusion) | copy-start | bytes 1769476
where the time goes:
time: 104 us
  Pallas kernels  62.4 us (60%)
  starting transfers between devices  17.8 us (17%)
  matrix products  5.68 us (5%)
  waiting for transfers between devices  5.33 us (5%)
  local copies, waits for them, and re-layouts  4.9 us (5%)
  other arithmetic  4.43 us (4%)
  between operations  3.51 us (3%)
    pallas_call x1, Pallas kernels, total_over_slabs(): pl.pallas_call(total_kernel, out_shape=jax.ShapeDtypeStruct((1, lanes), j...  38.4 us
    pallas_call x4, Pallas kernels, sum_edges(): pl.pallas_call(functools.partial(edge_kernel, column=column, block=block,...  21.4 us
    ppermute x4, starting transfers between devices, passed_along(): lax.ppermute(array, axis, [(i, (i + by) % devices) for i in range(devices)])  12.7 us
    ppermute x2, waiting for transfers between devices, local(): other = lax.ppermute(aggregated, 'chan', [(0, 1), (1, 0)])  5.32 us
    ppermute x2, starting transfers between devices, local(): other = lax.ppermute(aggregated, 'chan', [(0, 1), (1, 0)])  5.09 us
    pallas_call x2, Pallas kernels, radial_net(): pl.pallas_call(functools.partial(radial_kernel, column=column, block=min(...  2.62 us
    unnamed x32, local copies, waits for them, and re-layouts  2.32 us
  transfers between devices with their start and end apart: 6, of which 2 were waited for; matrix products, arithmetic and copies ran while one was open for 3% of the time, Pallas kernels for 15%

commit v1 on v0

--- a/solution.py
+++ b/solution.py
@@ -22,30 +22,95 @@
     return lax.ppermute(array, axis, [(i, (i + by) % devices) for i in range(devices)])
 
 
-def mix_channels(weights, rounded):
-    scalar_part = jnp.dot(weights[0], rounded[0], preferred_element_type=jnp.float32)[None]
-    vector_part = jnp.einsum(
-        "oi,kia->koa", weights[1], rounded[1:4], preferred_element_type=jnp.float32
-    )
-    tensor_part = jnp.einsum(
-        "oi,kia->koa", weights[2], rounded[4:9], preferred_element_type=jnp.float32
-    )
-    return jnp.concatenate([scalar_part, vector_part, tensor_part], axis=0)
-
-
-def gate_update(aggregated, scalar_weight, irrep_weight):
-    channels = aggregated.shape[1]
-    mixed_scalar = jnp.dot(scalar_weight, aggregated[0], preferred_element_type=jnp.float32)
-    mixed_vector = jnp.einsum(
-        "oi,kia->koa", irrep_weight[0], aggregated[1:4], preferred_element_type=jnp.float32
-    )
-    mixed_tensor = jnp.einsum(
-        "oi,kia->koa", irrep_weight[1], aggregated[4:9], preferred_element_type=jnp.float32
-    )
-    new_scalar = jax.nn.silu(mixed_scalar[:channels])[None]
-    new_vector = jax.nn.sigmoid(mixed_scalar[channels : 2 * channels])[None] * mixed_vector
-    new_tensor = jax.nn.sigmoid(mixed_scalar[2 * channels :])[None] * mixed_tensor
-    return jnp.concatenate([new_scalar, new_vector, new_tensor], axis=0)
+def kind_of(component):
+    return 0 if component == 0 else 1 if component < 4 else 2
+
+
+def mix_and_choose(state_ref, mix_ref, halo_ref, layer, table_ref, left_ref, right_ref):
+    channels = mix_ref.shape[2]
+    atoms = table_ref.shape[1]
+    for k in range(9):
+        table_ref[k * channels : (k + 1) * channels, :] = jnp.dot(
+            mix_ref[layer, kind_of(k)],
+            state_ref[k].astype(jnp.bfloat16),
+            preferred_element_type=jnp.float32,
+        ).astype(jnp.bfloat16)
+    for side, out_ref in ((0, left_ref), (1, right_ref)):
+        chosen = halo_ref[0, side : side + 1, :]
+        names = lax.broadcasted_iota(jnp.int32, (atoms, chosen.shape[1]), 0)
+        onehot = jnp.where(names == chosen, 1.0, 0.0).astype(jnp.bfloat16)
+        out_ref[...] = jnp.dot(
+            table_ref[...], onehot, preferred_element_type=jnp.float32
+        ).astype(jnp.bfloat16)
+
+
+def start_kernel(
+    species_ref, embed_ref, mix_ref, halo_ref, state_ref, table_ref, left_ref, right_ref
+):
+    species = species_ref[...]
+    embed = embed_ref[...].astype(jnp.float32)
+    scalar = jnp.zeros(state_ref.shape[1:], jnp.float32)
+    for kind in range(embed.shape[1]):
+        scalar = scalar + jnp.where(species == kind, embed[:, kind : kind + 1], 0.0)
+    state_ref[0] = scalar
+    state_ref[1:] = jnp.zeros((8, *scalar.shape), jnp.float32)
+    mix_and_choose(state_ref, mix_ref, halo_ref, 0, table_ref, left_ref, right_ref)
+
+
+def update_state(own_ref, other_ref, old_ref, scalar_ref, irrep_ref, new_ref, all_sc, layer):
+    channels = own_ref.shape[0] // 9
+    wide = old_ref.shape[1]
+    me = lax.axis_index("chan")
+    for k in range(9):
+        for part, ref in ((me, own_ref), (1 - me, other_ref)):
+            place = pl.ds(pl.multiple_of(part * channels, channels), channels)
+            all_sc[k, place, :] = ref[k * channels : (k + 1) * channels, :]
+    mixed = 0.5 * jnp.dot(scalar_ref[layer], all_sc[0], preferred_element_type=jnp.float32)
+    new_ref[0] = old_ref[0] + silu_of_twice(mixed[0:wide])
+    gates = 0.5 * jnp.tanh(mixed[wide:]) + 0.5
+    for k in range(1, 9):
+        kind = kind_of(k) - 1
+        value = jnp.dot(irrep_ref[layer, kind], all_sc[k], preferred_element_type=jnp.float32)
+        new_ref[k] = old_ref[k] + gates[kind * wide : (kind + 1) * wide] * value
+
+
+def middle_kernel(
+    own_ref, other_ref, old_ref, scalar_ref, irrep_ref, mix_ref, halo_ref, *rest, layer
+):
+    new_ref, table_ref, left_ref, right_ref, all_sc = rest
+    update_state(own_ref, other_ref, old_ref, scalar_ref, irrep_ref, new_ref, all_sc, layer)
+    mix_and_choose(new_ref, mix_ref, halo_ref, layer + 1, table_ref, left_ref, right_ref)
+
+
+def final_kernel(
+    atom_ref, base_ref, own_ref, other_ref, old_ref, scalar_ref, irrep_ref, *rest, layer
+):
+    readout_ref, species_ref, new_ref, energy_ref, part_ref, all_sc = rest
+    update_state(own_ref, other_ref, old_ref, scalar_ref, irrep_ref, new_ref, all_sc, layer)
+    energy = jnp.sum(new_ref[0] * readout_ref[...], axis=0, keepdims=True)
+    species = species_ref[...]
+    for kind in range(base_ref.shape[0]):
+        energy = energy + jnp.where(species == kind, base_ref[kind], 0.0)
+    place = lax.broadcasted_iota(jnp.int32, energy.shape, 1)
+    energy = jnp.where(place < atom_ref[0], energy, 0.0)
+    energy_ref[...] = energy
+    part = energy[:, 0:128]
+    for lane in range(128, energy.shape[1], 128):
+        part = part + energy[:, lane : lane + 128]
+    part_ref[...] = part
+
+
+def node_call(kernel, scalars, arrays, shapes, gathered=None):
+    in_vmem = pl.BlockSpec(memory_space=pltpu.VMEM)
+    return pl.pallas_call(
+        kernel,
+        out_shape=tuple(jax.ShapeDtypeStruct(*shape) for shape in shapes),
+        in_specs=[pl.BlockSpec(memory_space=pltpu.SMEM)] * len(scalars) + [in_vmem] * len(arrays),
+        out_specs=(in_vmem,) * len(shapes),
+        scratch_shapes=[] if gathered is None else [pltpu.VMEM(gathered, jnp.bfloat16)],
+        compiler_params=pltpu.CompilerParams(vmem_limit_bytes=20 * 2**20),
+        cost_estimate=pl.CostEstimate(flops=10**9, bytes_accessed=2 * 10**6, transcendentals=0),
+    )(*scalars, *arrays)
 
 
 def sine_of_pi_times(turns):
@@ -67,51 +132,67 @@
     return half + half * jnp.tanh(half)
 
 
-def radial_kernel(count_ref, vec_ref, first_ref, middle_ref, hidden_ref, unit_ref, *, column, block):
+def radial_kernel(
+    count_ref, inner_ref, outer_ref, first_ref, middle_ref, *outs, block
+):
     orders = (lax.broadcasted_iota(jnp.int32, (8, 1), 0) + 1).astype(jnp.float32)
-
-    def visit(index, carry):
-        span = pl.ds(pl.multiple_of(index * block, block), block)
-        vec = vec_ref[:, span]
-        x, y, z = vec[0:1], vec[1:2], vec[2:3]
-        squared = x * x + y * y + z * z
-        length = jnp.sqrt(squared)
-        inverse = lax.rsqrt(squared + 0.25)
-        fraction = jnp.minimum(length * (1.0 / cutoff), 1.0)
-        cubed = fraction * fraction * fraction
-        envelope = 1.0 + cubed * cubed * (-28.0 + fraction * (48.0 - 21.0 * fraction))
-        height = math.sqrt(2.0 / cutoff) * inverse * envelope
-        bessel = sine_of_pi_times(orders * (length * (1.0 / cutoff))) * height
-        unit_ref[0:1, span] = x * inverse
-        unit_ref[1:2, span] = y * inverse
-        unit_ref[2:3, span] = z * inverse
-        hidden = silu_of_twice(
-            jnp.dot(first_ref[...], bessel.astype(jnp.bfloat16), preferred_element_type=jnp.float32)
-        ).astype(jnp.bfloat16)
-        hidden_ref[:, span] = silu_of_twice(
-            jnp.dot(middle_ref[...], hidden, preferred_element_type=jnp.float32)
-        ).astype(jnp.bfloat16)
-        return carry
-
-    lax.fori_loop(0, (count_ref[0, column] + block - 1) // block, visit, 0)
-
-
-def radial_net(edge_count, vec, first, middle, column):
-    slots = vec.shape[1]
+    layers, breadth, _ = first_ref.shape
+
+    def visit_list(column, vec_ref, hidden_ref, unit_ref):
+        def visit(index, carry):
+            span = pl.ds(pl.multiple_of(index * block, block), block)
+            vec = vec_ref[:, span]
+            x, y, z = vec[0:1], vec[1:2], vec[2:3]
+            squared = x * x + y * y + z * z
+            length = jnp.sqrt(squared)
+            inverse = lax.rsqrt(squared + 0.25)
+            fraction = jnp.minimum(length * (1.0 / cutoff), 1.0)
+            cubed = fraction * fraction * fraction
+            envelope = 1.0 + cubed * cubed * (-28.0 + fraction * (48.0 - 21.0 * fraction))
+            height = math.sqrt(2.0 / cutoff) * inverse * envelope
+            bessel = sine_of_pi_times(orders * (length * (1.0 / cutoff))) * height
+            bessel = bessel.astype(jnp.bfloat16)
+            unit_ref[0:1, span] = x * inverse
+            unit_ref[1:2, span] = y * inverse
+            unit_ref[2:3, span] = z * inverse
+            hidden = [
+                silu_of_twice(
+                    0.5 * jnp.dot(first_ref[k], bessel, preferred_element_type=jnp.float32)
+                ).astype(jnp.bfloat16)
+                for k in range(layers)
+            ]
+            for k in range(layers):
+                hidden_ref[k * breadth : (k + 1) * breadth, span] = silu_of_twice(
+                    0.5 * jnp.dot(middle_ref[k], hidden[k], preferred_element_type=jnp.float32)
+                ).astype(jnp.bfloat16)
+            return carry
+
+        lax.fori_loop(0, (count_ref[0, column] + block - 1) // block, visit, 0)
+
+    visit_list(0, inner_ref, *outs[0:2])
+    visit_list(1, outer_ref, *outs[2:4])
+
+
+def radial_net(edge_count, inner_vec, outer_vec, first, middle):
     in_vmem = pl.BlockSpec(memory_space=pltpu.VMEM)
+    shapes = []
+    for vec in (inner_vec, outer_vec):
+        slots = vec.shape[1]
+        shapes.append(
+            jax.ShapeDtypeStruct((middle.shape[0] * middle.shape[1], slots), jnp.bfloat16)
+        )
+        shapes.append(jax.ShapeDtypeStruct((8, slots), jnp.float32))
+    slots = inner_vec.shape[1] + outer_vec.shape[1]
     return pl.pallas_call(
-        functools.partial(radial_kernel, column=column, block=min(2048, slots)),
-        out_shape=(
-            jax.ShapeDtypeStruct((middle.shape[0], slots), jnp.bfloat16),
-            jax.ShapeDtypeStruct((8, slots), jnp.float32),
-        ),
-        in_specs=[pl.BlockSpec(memory_space=pltpu.SMEM)] + [in_vmem] * 3,
-        out_specs=(in_vmem, in_vmem),
+        functools.partial(radial_kernel, block=min(2048, outer_vec.shape[1])),
+        out_shape=tuple(shapes),
+        in_specs=[pl.BlockSpec(memory_space=pltpu.SMEM)] + [in_vmem] * 4,
+        out_specs=(in_vmem,) * 4,
         compiler_params=pltpu.CompilerParams(vmem_limit_bytes=40 * 2**20),
         cost_estimate=pl.CostEstimate(
             flops=slots * 40000, bytes_accessed=slots * 300, transcendentals=0
         ),
-    )(edge_count, vec, first, middle)
+    )(edge_count, inner_vec, outer_vec, first, middle)
 
 
 def edge_kernel(
@@ -125,7 +206,7 @@
     column,
     block,
     channels,
-    first_row,
+    layer,
     last,
 ):
     if last:
@@ -138,7 +219,8 @@
     blocks = (count + block - 1) // block
     slots = edges_ref.shape[1]
     rows, atoms = table_ref.shape
-    breadth = mix_ref.shape[1]
+    breadth = mix_ref.shape[3]
+    first_row = layer * breadth
     sum_sc[...] = jnp.zeros_like(sum_sc)
     message_sc[1][...] = jnp.zeros_like(message_sc[1])
     names = lax.broadcasted_iota(jnp.int32, (atoms, 1), 0).astype(jnp.float32).astype(jnp.bfloat16)
@@ -165,7 +247,9 @@
         def weigh(lane):
             cut = slice(lane, lane + 256)
             weight_sc[into][:, cut] = jnp.dot(
-                mix_ref[...], hidden[:, cut], preferred_element_type=jnp.float32
+                mix_ref[layer].reshape(-1, breadth),
+                hidden[:, cut],
+                preferred_element_type=jnp.float32,
             )
 
         lanes = range(0, block, 256)
@@ -277,7 +361,7 @@
     slots = edges.shape[1]
     last = before is not None
     block = min(512 if last else 1024, slots)
-    paths, breadth = mix.shape
+    paths = mix.shape[1] * mix.shape[2]
     in_vmem = pl.BlockSpec(memory_space=pltpu.VMEM)
     arrays = [edge_count, table, edges, hidden, unit, mix]
     if last:
@@ -292,7 +376,7 @@
             column=column,
             block=block,
             channels=rows // 9,
-            first_row=layer_index * breadth,
+            layer=layer_index,
             last=last,
         ),
         out_shape=jax.ShapeDtypeStruct((rows, atoms), jnp.bfloat16 if last else jnp.float32),
@@ -310,7 +394,9 @@
     )(*arrays)
 
 
-def total_kernel(part_ref, total_ref, near_sc, far_sc, near_send, near_recv, far_send, far_recv):
+def total_kernel(
+    part_ref, mean_ref, near_sc, far_sc, near_send, near_recv, far_send, far_recv, *, scale
+):
     far, *near = SLAB
     sizes = [lax.axis_size(name) for name in near]
     place = [lax.axis_index(name) for name in near]
@@ -374,21 +460,21 @@
     far_sc[far_place] = near_sc[...]
     for step in range(1, far_size):
         far_copy(step, (far_place + far_size - step) % far_size).wait_recv()
-    total_ref[...] = jnp.sum(far_sc[...], axis=(0, 1))
+    mean_ref[0, 0] = jnp.sum(far_sc[...]) * scale
     for step in range(1, near_total):
         near_copy(step, mine).wait_send()
     for step in range(1, far_size):
         far_copy(step, far_place).wait_send()
 
 
-def total_over_slabs(part):
+def mean_over_slabs(part, scale):
     lanes = part.shape[1]
     far_size, near_total = lax.axis_size(SLAB[0]), lax.axis_size(SLAB[1:])
     return pl.pallas_call(
-        total_kernel,
-        out_shape=jax.ShapeDtypeStruct((1, lanes), jnp.float32),
+        functools.partial(total_kernel, scale=scale),
+        out_shape=jax.ShapeDtypeStruct((1, 1), jnp.float32),
         in_specs=[pl.BlockSpec(memory_space=pltpu.VMEM)],
-        out_specs=pl.BlockSpec(memory_space=pltpu.VMEM),
+        out_specs=pl.BlockSpec(memory_space=pltpu.SMEM),
         scratch_shapes=[
             pltpu.VMEM((near_total, 1, lanes), jnp.float32),
             pltpu.VMEM((far_size, near_total, 1, lanes), jnp.float32),
@@ -421,60 +507,49 @@
     species_energy,
 ):
     atom_total = species.shape[0]
-    species_total = embed_table.shape[1]
-    onehot = species[None, :] == jnp.arange(species_total, dtype=jnp.int32)[:, None]
-    scalar_init = jnp.dot(
-        embed_table, onehot.astype(jnp.bfloat16), preferred_element_type=jnp.float32
+    wide, channels = embed_table.shape[0], mix_in.shape[2]
+    rows = 9 * channels
+    state_shape = ((9, wide, atom_total), jnp.float32)
+    table_shapes = [((rows, atom_total), jnp.bfloat16)]
+    table_shapes += [((rows, halo_index.shape[2]), jnp.bfloat16)] * 2
+    gathered = (9, wide, atom_total)
+    species = species[None]
+    layers = radial_in.shape[0]
+    node_state, table, to_left, to_right = node_call(
+        start_kernel,
+        [],
+        [species, embed_table, mix_in, halo_index],
+        [state_shape, *table_shapes],
     )
-    node_state = jnp.concatenate(
-        [scalar_init[None], jnp.zeros((8,) + scalar_init.shape, jnp.float32)], axis=0
-    )
-    channels = mix_in.shape[2]
-    atom_slots = jnp.arange(atom_total, dtype=jnp.int32)
-    to_left, to_right = (
-        (atom_slots[:, None] == halo_index[0, side][None, :]).astype(jnp.bfloat16)
-        for side in (0, 1)
-    )
-    first = lax.axis_index("chan") == 0
-    layers, breadth, _ = radial_in.shape
-    first_weights = (radial_in * 0.5).reshape(layers * breadth, -1)
-    middle_weights = jnp.zeros((layers * breadth, layers * breadth), jnp.bfloat16)
-    for layer_index in range(layers):
-        cut = slice(layer_index * breadth, (layer_index + 1) * breadth)
-        middle_weights = middle_weights.at[cut, cut].set(radial_mid[layer_index] * 0.5)
-    for layer_index in range(layers):
-        rounded = node_state.astype(jnp.bfloat16)
-        features = mix_channels(mix_in[layer_index], rounded).astype(jnp.bfloat16)
-        table = features.reshape(9 * channels, atom_total)
-        mix = radial_out[layer_index].reshape(-1, breadth)
-
-        def boundary(choice):
-            return jnp.dot(table, choice, preferred_element_type=jnp.float32).astype(jnp.bfloat16)
-
-        from_left = passed_along(boundary(to_right), SLAB, 1)
-        from_right = passed_along(boundary(to_left), SLAB, -1)
-        if layer_index == 0:
-            inner_net = radial_net(edge_count, inner_vec, first_weights, middle_weights, 0)
-            outer_net = radial_net(edge_count, outer_vec, first_weights, middle_weights, 1)
-        summed = sum_edges(edge_count, table, inner_edges, *inner_net, mix, layer_index, 0)
+    nets = radial_net(edge_count, inner_vec, outer_vec, radial_in, radial_mid)
+    for layer in range(layers):
+        from_left = passed_along(to_right, SLAB, 1)
+        from_right = passed_along(to_left, SLAB, -1)
+        summed = sum_edges(edge_count, table, inner_edges, *nets[0:2], radial_out, layer, 0)
         halo_table = jnp.concatenate([from_left, from_right], axis=1)
-        aggregated = sum_edges(
-            edge_count, halo_table, outer_edges, *outer_net, mix, layer_index, 1, summed
-        ).reshape(9, channels, atom_total)
-        other = lax.ppermute(aggregated, "chan", [(0, 1), (1, 0)])
-        all_channels = jnp.concatenate(
-            [jnp.where(first, aggregated, other), jnp.where(first, other, aggregated)], axis=1
-        )
-        node_state = node_state + gate_update(
-            all_channels, mix_scalar[layer_index], mix_irrep[layer_index]
-        )
-    readout_part = jnp.sum(node_state[0] * readout[:, None], axis=0)
-    species_part = jnp.sum(onehot.astype(jnp.float32) * species_energy[:, None], axis=0)
-    live_atoms = (jnp.arange(atom_total, dtype=jnp.int32) < atom_count[0]).astype(jnp.float32)
-    atom_energy = (readout_part + species_part) * live_atoms
-    energy_sum = jnp.sum(total_over_slabs(jnp.sum(atom_energy.reshape(-1, 128), axis=0)[None]))
-    mean_energy = energy_sum / (atom_total * lax.axis_size(SLAB))
-    return (node_state, atom_energy, mean_energy)
+        own = sum_edges(
+            edge_count, halo_table, outer_edges, *nets[2:4], radial_out, layer, 1, summed
+        )
+        other = lax.ppermute(own, "chan", [(0, 1), (1, 0)])
+        arrays = [own, other, node_state, mix_scalar, mix_irrep]
+        if layer + 1 < layers:
+            node_state, table, to_left, to_right = node_call(
+                functools.partial(middle_kernel, layer=layer),
+                [],
+                [*arrays, mix_in, halo_index],
+                [state_shape, *table_shapes],
+                gathered,
+            )
+        else:
+            node_state, atom_energy, part = node_call(
+                functools.partial(final_kernel, layer=layer),
+                [atom_count, species_energy],
+                [*arrays, readout[:, None], species],
+                [state_shape, ((1, atom_total), jnp.float32), ((1, 128), jnp.float32)],
+                gathered,
+            )
+    mean = mean_over_slabs(part, 1.0 / (atom_total * lax.axis_size(SLAB)))
+    return (node_state, atom_energy[0], mean[0, 0])
 
 
 def solution(mesh):

time: 104 us -> 95.8 us (0.921)
  Pallas kernels: 62.4 us -> 71.8 us
  matrix products: 5.68 us -> 0 us
  starting transfers between devices: 17.8 us -> 12.3 us
  other arithmetic: 4.43 us -> 0.04 us
    pallas_call x4, Pallas kernels: 21.4 us -> 39.4 us  [sum_edges(): pl.pallas_call(functools.partial(edge_kernel, column=column, block=block,...]
    pallas_call x3 -> x5, Pallas kernels: 41 us -> 32.4 us  [the longest x1 25.4 us: mean_over_slabs(): pl.pallas_call(functools.partial(total_kernel, scale=scale), out_shape=ja...]
    dot_general x17 -> x0, matrix products: 5.68 us -> none  [the longest x2 1 us: mix_channels(): jnp.einsum('oi,kia->koa', weights[2], rounded[4:9], preferred_element_typ...]
    ppermute x4, starting transfers between devices: 12.7 us -> 7.29 us  [passed_along(): lax.ppermute(array, axis, [(i, (i + by) % devices) for i in range(devices)])]
    reduce_sum x4 -> x0, other arithmetic: 2.06 us -> none  [the longest x1 1.28 us: local(): jnp.sum(total_over_slabs(jnp.sum(atom_energy.reshape(-1, 128), axis=0)[No...]
    mul x3 -> x0, other arithmetic: 1.99 us -> none  [the longest x1 0.74 us: local(): radial_mid[layer_index] * 0.5]
    unnamed x32 -> x49, local copies, waits for them, and re-layouts: 2.32 us -> 3.83 us
  transfers between devices with their start and end apart: 6 -> 6, of which waited for: 2 -> 2; matrix products, arithmetic and copies ran while one was open for 3% -> 0% of each run, Pallas kernels for 15% -> 38%
where the time goes in v1:
time: 95.8 us; the launch traced here: 96.7 us
  Pallas kernels  71.8 us (75%)
  starting transfers between devices  12.3 us (13%)
  waiting for transfers between devices  5.29 us (6%)
  local copies, waits for them, and re-layouts  3.92 us (4%)
  between operations  3.3 us (3%)
    pallas_call x4, Pallas kernels, sum_edges(): pl.pallas_call(functools.partial(edge_kernel, column=column, block=block,...  39.4 us
    pallas_call x1, Pallas kernels, mean_over_slabs(): pl.pallas_call(functools.partial(total_kernel, scale=scale), out_shape=ja...  25.4 us
    ppermute x4, starting transfers between devices, passed_along(): lax.ppermute(array, axis, [(i, (i + by) % devices) for i in range(devices)])  7.29 us
    ppermute x2, waiting for transfers between devices, local(): other = lax.ppermute(own, 'chan', [(0, 1), (1, 0)])  5.28 us
    ppermute x2, starting transfers between devices, local(): other = lax.ppermute(own, 'chan', [(0, 1), (1, 0)])  5 us
    pallas_call x1, Pallas kernels, radial_net(): pl.pallas_call(functools.partial(radial_kernel, block=min(2048, outer_vec...  4.45 us
    unnamed x49, local copies, waits for them, and re-layouts  3.83 us
    pallas_call x3, Pallas kernels, node_call(): pl.pallas_call(kernel, out_shape=tuple((jax.ShapeDtypeStruct(*shape) for...  2.6 us
  transfers between devices with their start and end apart: 6, of which 2 were waited for; matrix products, arithmetic and copies ran while one was open for 0% of the time, Pallas kernels for 38%

profile of v1, /device:TPU:1, one launch (start us, length us, event | category | flops | bytes accessed | tf_op | source)
XLA Modules:
  0.0 96.7 jit_solution(1927885958291346342)
XLA Ops:
  0.7 0.8 copy.20.embed_ref
  1.5 0.8 copy-done.5
  2.3 0.7 copy-done.9
  3.0 0.7 copy-done.11
  3.7 0.4 shard_map.184
  4.1 2.7 %collective-permute-start = (bf16[288,128]{1,0:T(8,128)(2,1)S(1)}, bf16[288,128]{1,0:T(8,128)(2,1)S(1)}, u32[]{:S(2)}, u32[]{:S(2)}) collective-permute-start(bf16[288,128]{1,0:T(8,128)(2,1)S(1)} %get-tuple-element.18), channel_id=1, source_target_pairs={{0,2},{2,4},{4,6},{6,8},{8,10},{10,12},{12,14},{14,16},{16,18},{18... | collective-permute-start | bytes 221192 | tf_op jit(solution)/shard_map/ppermute | solution.py:22
  6.8 0.7 collective-permute-start.1
  7.5 0.1 copy.21.first_ref
  7.6 4.5 %shard_map.185 = (bf16[128,12288]{1,0:T(8,128)(2,1)S(1)}, f32[8,12288]{1,0:T(8,128)S(1)}, bf16[128,4096]{1,0:T(8,128)(2,1)S(1)}, f32[8,4096]{1,0:T(8,128)S(1)}) custom-call(s32[1,2]{1,0:T(1,128)S(1)} %copy-done.13, f32[3,12288]{1,0:T(4,128)S(1)} %copy-done, f32[3,4096]{1,0:T(4,128)S(1)} %copy-done.3, bf16[2,64,8]{2,1,0:T(8,128)(2,1)S(1)} %copy.21.first_ref, ...), custom_call_target="tpu_custom_call" | custom-call | flops 655360000 | bytes 4915200 | tf_op jit(solution)/shard_map/pallas_call | solution.py:186
  12.1 0.0 copy-start.18
  12.1 0.0 copy-start.8
  12.1 16.3 %shard_map.186.rest_0_ = f32[288,256]{1,0:T(8,128)S(1)} custom-call(s32[1,2]{1,0:T(1,128)S(1)} %copy-done.13, bf16[288,256]{1,0:T(8,128)(2,1)S(1)} %get-tuple-element.22.table_ref, s32[2,12288]{1,0:T(2,128)S(1)} %copy-done.2, bf16[128,12288]{1,0:T(8,128)(2,1)S(1)} %get-tuple-element.23.hidden_ref, f32[8,12288]{1,0:T(8,128)S(1)} %get-tuple-element.24.unit_ref, ...), custom_call_target="tpu_custom_call" | custom-call | flops 4915200000 | bytes 3686400 | tf_op jit(solution)/shard_map/pallas_call | solution.py:373
  28.4 0.0 copy-start.20
  28.5 0.0 copy-start.4
  28.5 0.0 copy-start.6
  28.5 3.4 %shard_map.187.own_ref = bf16[288,256]{1,0:T(8,128)(2,1)S(1)} custom-call(s32[1,2]{1,0:T(1,128)S(1)} %copy-done.13, bf16[288,256]{1,0:T(8,128)(2,1)S(1)} %pad_maximum_fusion.table_ref, s32[2,4096]{1,0:T(2,128)S(1)} %copy-done.8, bf16[128,4096]{1,0:T(8,128)(2,1)S(1)} %get-tuple-element.20.hidden_ref, f32[8,4096]{1,0:T(8,128)S(1)} %get-tuple-element.21.unit_ref, ...), custom_call_target="tpu_custom_call" | custom-call | flops 1638400000 | bytes 1228800 | tf_op jit(solution)/shard_map/pallas_call | solution.py:373
  31.9 2.3 %collective-permute-start.2 = (bf16[288,256]{1,0:T(8,128)(2,1)S(1)}, bf16[288,256]{1,0:T(8,128)(2,1)S(1)}, u32[]{:S(2)}, u32[]{:S(2)}) collective-permute-start(bf16[288,256]{1,0:T(8,128)(2,1)S(1)} %shard_map.187.own_ref), channel_id=1, source_target_pairs={{0,1},{1,0},{2,3},{3,2},{4,5},{5,4},{6,7},{7,6},{8,9},{9,8},{10,11... | collective-permute-start | bytes 442376 | tf_op jit(solution)/shard_map/ppermute | solution.py:533
  34.2 0.1 copy.22.scalar_ref
  34.3 3.1 %collective-permute-done.2.other_ref = bf16[288,256]{1,0:T(8,128)(2,1)S(1)} collective-permute-done((bf16[288,256]{1,0:T(8,128)(2,1)S(1)}, bf16[288,256]{1,0:T(8,128)(2,1)S(1)}, u32[]{:S(2)}, u32[]{:S(2)}) %collective-permute-start.2) | collective-permute-done | bytes 147488 | tf_op jit(solution)/shard_map/ppermute | solution.py:533
  37.5 0.6 shard_map.188
  38.1 0.1 collective-permute-start.3
  38.2 3.8 %collective-permute-start.4 = (bf16[288,128]{1,0:T(8,128)(2,1)S(1)}, bf16[288,128]{1,0:T(8,128)(2,1)S(1)}, u32[]{:S(2)}, u32[]{:S(2)}) collective-permute-start(bf16[288,128]{1,0:T(8,128)(2,1)S(1)} %get-tuple-element.27), channel_id=1, source_target_pairs={{0,254},{2,0},{4,2},{6,4},{8,6},{10,8},{12,10},{14,12},{16,14},{18... | collective-permute-start | bytes 221192 | tf_op jit(solution)/shard_map/ppermute | solution.py:22
  42.0 16.4 %shard_map.189.rest_0_ = f32[288,256]{1,0:T(8,128)S(1)} custom-call(s32[1,2]{1,0:T(1,128)S(1)} %copy-done.13, bf16[288,256]{1,0:T(8,128)(2,1)S(1)} %get-tuple-element.28.table_ref, s32[2,12288]{1,0:T(2,128)S(1)} %copy-done.2, bf16[128,12288]{1,0:T(8,128)(2,1)S(1)} %copy-done.17, f32[8,12288]{1,0:T(8,128)S(1)} %get-tuple-element.24.unit_ref, ...), custom_call_target="tpu_custom_call" | custom-call | flops 4915200000 | bytes 3686400 | tf_op jit(solution)/shard_map/pallas_call | solution.py:373
  58.4 0.0 copy-start.12
  58.4 0.0 copy-start.14
  58.5 3.4 %shard_map.190.own_ref = bf16[288,256]{1,0:T(8,128)(2,1)S(1)} custom-call(s32[1,2]{1,0:T(1,128)S(1)} %copy-done.13, bf16[288,256]{1,0:T(8,128)(2,1)S(1)} %pad_maximum_fusion.1.table_ref, s32[2,4096]{1,0:T(2,128)S(1)} %copy-done.8, bf16[128,4096]{1,0:T(8,128)(2,1)S(1)} %get-tuple-element.20.hidden_ref, f32[8,4096]{1,0:T(8,128)S(1)} %copy-done.19, ...), custom_call_target="tpu_custom_call" | custom-call | flops 1638400000 | bytes 1228800 | tf_op jit(solution)/shard_map/pallas_call | solution.py:373
  61.9 2.7 %collective-permute-start.5 = (bf16[288,256]{1,0:T(8,128)(2,1)S(1)}, bf16[288,256]{1,0:T(8,128)(2,1)S(1)}, u32[]{:S(2)}, u32[]{:S(2)}) collective-permute-start(bf16[288,256]{1,0:T(8,128)(2,1)S(1)} %shard_map.190.own_ref), channel_id=1, source_target_pairs={{0,1},{1,0},{2,3},{3,2},{4,5},{5,4},{6,7},{7,6},{8,9},{9,8},{10,11... | collective-permute-start | bytes 442376 | tf_op jit(solution)/shard_map/ppermute | solution.py:533
  64.6 0.1 copy.24.rest_0_
  65.3 2.1 %collective-permute-done.5.other_ref = bf16[288,256]{1,0:T(8,128)(2,1)S(1)} collective-permute-done((bf16[288,256]{1,0:T(8,128)(2,1)S(1)}, bf16[288,256]{1,0:T(8,128)(2,1)S(1)}, u32[]{:S(2)}, u32[]{:S(2)}) %collective-permute-start.5) | collective-permute-done | bytes 147488 | tf_op jit(solution)/shard_map/ppermute | solution.py:533
  67.5 1.6 %shard_map.191 = (f32[9,64,256]{2,1,0:T(8,128)}, f32[1,256]{1,0:T(1,128)}, f32[1,128]{1,0:T(1,128)S(1)}) custom-call(s32[1]{0:T(128)S(6)} %copy.26.atom_ref, f32[5]{0:T(128)S(1)} %copy-done.14, bf16[288,256]{1,0:T(8,128)(2,1)S(1)} %shard_map.190.own_ref, bf16[288,256]{1,0:T(8,128)(2,1)S(1)} %collective-permute-done.5.other_ref, ...), custom_call_target="tpu_custom_call" | custom-call | flops 1000000000 | bytes 2000000 | tf_op jit(solution)/shard_map/pallas_call | solution.py:105
  69.1 0.5 copy-done.15
  69.6 25.4 %shard_map.192 = f32[1,1]{1,0:T(1,128)} custom-call(f32[1,128]{1,0:T(1,128)} %copy-done.15), custom_call_target="tpu_custom_call" | custom-call | tf_op jit(solution)/shard_map/pallas_call | solution.py:473
  (41 shorter events, 0.1 us)
Async XLA Ops:
  0.6 7.0 %copy-start = (f32[3,12288]{1,0:T(4,128)S(1)}, f32[3,12288]{1,0:T(4,128)}, u32[]{:S(2)}) copy-start(f32[3,12288]{1,0:T(4,128)} %inner_ref.1) | copy-start | bytes 442372
  0.6 7.0 %copy-start.3 = (f32[3,4096]{1,0:T(4,128)S(1)}, f32[3,4096]{1,0:T(4,128)}, u32[]{:S(2)}) copy-start(f32[3,4096]{1,0:T(4,128)} %outer_ref.1) | copy-start | bytes 147460
  0.7 11.5 %copy-start.2 = (s32[2,12288]{1,0:T(2,128)S(1)}, s32[2,12288]{1,0:T(2,128)}, u32[]{:S(2)}) copy-start(s32[2,12288]{1,0:T(2,128)} %edges_ref.6) | copy-start | bytes 294916
  0.7 11.5 %copy-start.1 = (bf16[2,10,32,64]{3,2,1,0:T(8,128)(2,1)S(1)}, bf16[2,10,32,64]{3,2,1,0:T(8,128)(2,1)}, u32[]{:S(2)}) copy-start(bf16[2,10,32,64]{3,2,1,0:T(8,128)(2,1)} %mix_ref.11) | copy-start | bytes 245764
  1.5 0.8 copy-start.5
  2.3 0.7 copy-start.9
  3.0 0.7 copy-start.11
  3.7 3.8 %copy-start.21 = (bf16[2,64,8]{1,2,0:T(8,128)(2,1)S(1)}, bf16[2,64,8]{1,2,0:T(8,128)(2,1)}, u32[]{:S(2)}) copy-start(bf16[2,64,8]{1,2,0:T(8,128)(2,1)} %param.26) | copy-start | bytes 6148
  3.7 3.9 %copy-start.7 = (bf16[2,64,64]{2,1,0:T(8,128)(2,1)S(1)}, bf16[2,64,64]{2,1,0:T(8,128)(2,1)}, u32[]{:S(2)}) copy-start(bf16[2,64,64]{2,1,0:T(8,128)(2,1)} %middle_ref.1) | copy-start | bytes 49156
  3.7 3.9 %copy-start.13 = (s32[1,2]{1,0:T(1,128)S(1)}, s32[1,2]{1,0:T(1,128)}, u32[]{:S(2)}) copy-start(s32[1,2]{1,0:T(1,128)} %count_ref.9) | copy-start | bytes 28
  4.1 24.3 %collective-permute-start = (bf16[288,128]{1,0:T(8,128)(2,1)S(1)}, bf16[288,128]{1,0:T(8,128)(2,1)S(1)}, u32[]{:S(2)}, u32[]{:S(2)}) collective-permute-start(bf16[288,128]{1,0:T(8,128)(2,1)S(1)} %get-tuple-element.18), channel_id=1, source_target_pairs={{0,2},{2,4},{4,6},{6,8},{8,10},{10,12},{12,14},{14,16},{16,18},{18... | collective-permute-start | bytes 221192 | tf_op jit(solution)/shard_map/ppermute | solution.py:22
  6.8 21.7 %collective-permute-start.1 = (bf16[288,128]{1,0:T(8,128)(2,1)S(1)}, bf16[288,128]{1,0:T(8,128)(2,1)S(1)}, u32[]{:S(2)}, u32[]{:S(2)}) collective-permute-start(bf16[288,128]{1,0:T(8,128)(2,1)S(1)} %get-tuple-element.19), channel_id=1, source_target_pairs={{0,254},{2,0},{4,2},{6,4},{8,6},{10,8},{12,10},{14,12},{16,14},{18... | collective-permute-start | bytes 221192 | tf_op jit(solution)/shard_map/ppermute | solution.py:22
  12.1 16.3 %copy-start.16 = (bf16[128,12288]{1,0:T(8,128)(2,1)}, bf16[128,12288]{1,0:T(8,128)(2,1)S(1)}, u32[]{:S(2)}) copy-start(bf16[128,12288]{1,0:T(8,128)(2,1)S(1)} %get-tuple-element.23.hidden_ref) | copy-start | bytes 9437188
  12.1 16.4 %copy-start.18 = (f32[8,4096]{1,0:T(8,128)}, f32[8,4096]{1,0:T(8,128)S(1)}, u32[]{:S(2)}) copy-start(f32[8,4096]{1,0:T(8,128)S(1)} %get-tuple-element.21.unit_ref) | copy-start | bytes 393220
  12.1 16.4 %copy-start.8 = (s32[2,4096]{1,0:T(2,128)S(1)}, s32[2,4096]{1,0:T(2,128)}, u32[]{:S(2)}) copy-start(s32[2,4096]{1,0:T(2,128)} %edges_ref.7) | copy-start | bytes 98308
  28.4 5.8 %copy-start.20 = (bf16[2,192,64]{1,2,0:T(8,128)(2,1)S(1)}, bf16[2,192,64]{1,2,0:T(8,128)(2,1)}, u32[]{:S(2)}) copy-start(bf16[2,192,64]{1,2,0:T(8,128)(2,1)} %param.30) | copy-start | bytes 147460
  28.5 9.0 %copy-start.4 = (bf16[2,2,64,64]{3,2,1,0:T(8,128)(2,1)S(1)}, bf16[2,2,64,64]{3,2,1,0:T(8,128)(2,1)}, u32[]{:S(2)}) copy-start(bf16[2,2,64,64]{3,2,1,0:T(8,128)(2,1)} %irrep_ref.3) | copy-start | bytes 98308
  28.5 9.0 %copy-start.6 = (bf16[2,3,32,64]{3,2,1,0:T(8,128)(2,1)S(1)}, bf16[2,3,32,64]{3,2,1,0:T(8,128)(2,1)}, u32[]{:S(2)}) copy-start(bf16[2,3,32,64]{3,2,1,0:T(8,128)(2,1)} %mix_ref.9) | copy-start | bytes 73732
  28.5 9.0 %copy-start.10 = (s32[1,2,128]{2,1,0:T(2,128)S(1)}, s32[1,2,128]{2,1,0:T(2,128)}, u32[]{:S(2)}) copy-start(s32[1,2,128]{2,1,0:T(2,128)} %halo_ref.3) | copy-start | bytes 3076
  31.9 5.6 %collective-permute-start.2 = (bf16[288,256]{1,0:T(8,128)(2,1)S(1)}, bf16[288,256]{1,0:T(8,128)(2,1)S(1)}, u32[]{:S(2)}, u32[]{:S(2)}) collective-permute-start(bf16[288,256]{1,0:T(8,128)(2,1)S(1)} %shard_map.187.own_ref), channel_id=1, source_target_pairs={{0,1},{1,0},{2,3},{3,2},{4,5},{5,4},{6,7},{7,6},{8,9},{9,8},{10,11... | collective-permute-start | bytes 442376 | tf_op jit(solution)/shard_map/ppermute | solution.py:533
  34.3 7.7 %copy-start.17 = (bf16[128,12288]{1,0:T(8,128)(2,1)S(1)}, bf16[128,12288]{1,0:T(8,128)(2,1)}, u32[]{:S(2)}) copy-start(bf16[128,12288]{1,0:T(8,128)(2,1)} %copy-done.16) | copy-start | bytes 9437188
  38.1 20.4 %collective-permute-start.3 = (bf16[288,128]{1,0:T(8,128)(2,1)S(1)}, bf16[288,128]{1,0:T(8,128)(2,1)S(1)}, u32[]{:S(2)}, u32[]{:S(2)}) collective-permute-start(bf16[288,128]{1,0:T(8,128)(2,1)S(1)} %get-tuple-element.26), channel_id=1, source_target_pairs={{0,2},{2,4},{4,6},{6,8},{8,10},{10,12},{12,14},{14,16},{16,18},{18... | collective-permute-start | bytes 221192 | tf_op jit(solution)/shard_map/ppermute | solution.py:22
  38.2 20.3 %collective-permute-start.4 = (bf16[288,128]{1,0:T(8,128)(2,1)S(1)}, bf16[288,128]{1,0:T(8,128)(2,1)S(1)}, u32[]{:S(2)}, u32[]{:S(2)}) collective-permute-start(bf16[288,128]{1,0:T(8,128)(2,1)S(1)} %get-tuple-element.27), channel_id=1, source_target_pairs={{0,254},{2,0},{4,2},{6,4},{8,6},{10,8},{12,10},{14,12},{16,14},{18... | collective-permute-start | bytes 221192 | tf_op jit(solution)/shard_map/ppermute | solution.py:22
  42.0 16.5 %copy-start.19 = (f32[8,4096]{1,0:T(8,128)S(1)}, f32[8,4096]{1,0:T(8,128)}, u32[]{:S(2)}) copy-start(f32[8,4096]{1,0:T(8,128)} %copy-done.18) | copy-start | bytes 393220
  58.4 6.2 %copy-start.22 = (f32[64]{0:T(128)S(1)}, f32[64]{0:T(128)}, u32[]{:S(2)}) copy-start(f32[64]{0:T(128)} %param.32) | copy-start | bytes 772
  58.4 9.0 %copy-start.12 = (s32[256]{0:T(256)S(1)}, s32[256]{0:T(256)}, u32[]{:S(2)}) copy-start(s32[256]{0:T(256)} %param.17) | copy-start | bytes 3076
  58.4 9.0 %copy-start.14 = (f32[5]{0:T(128)S(1)}, f32[5]{0:T(128)}, u32[]{:S(2)}) copy-start(f32[5]{0:T(128)} %base_ref.1) | copy-start | bytes 64
  61.9 5.6 %collective-permute-start.5 = (bf16[288,256]{1,0:T(8,128)(2,1)S(1)}, bf16[288,256]{1,0:T(8,128)(2,1)S(1)}, u32[]{:S(2)}, u32[]{:S(2)}) collective-permute-start(bf16[288,256]{1,0:T(8,128)(2,1)S(1)} %shard_map.190.own_ref), channel_id=1, source_target_pairs={{0,1},{1,0},{2,3},{3,2},{4,5},{5,4},{6,7},{7,6},{8,9},{9,8},{10,11... | collective-permute-start | bytes 442376 | tf_op jit(solution)/shard_map/ppermute | solution.py:533
  69.1 0.5 copy-start.15
